TPU v7x, 32 devices: a whole 2x2x4 slice. The times are simulated.
32 devices in a mesh: rows: 16 (over z, y, x), rhs: 2 (over core).
Axes of the slice: x: 2, y: 2, z: 4, core: 2. Of those that a mesh axis runs over, the one named last changes fastest.
Arguments:
- rhs: float32 [2, 8192, 4096], P(None, 'rows', 'rhs'), may hold values from -8 to 8
- factor: bfloat16 [2, 8192, 4, 512], P(None, 'rows', None, 'rhs'), may hold values from -0.125 to 0.125
- inverses: float32 [4, 512, 512], replicated, may hold values from -1 to 1, as said below
Outputs:
- state: float32 [2, 8192, 4096], P(None, 'rows', 'rhs')
Inputs may be any that keep to these rules, and one draw needn't show every extreme that they name: Each inverses[p] is unit lower triangular: ones on the diagonal, zeros above it.
All inputs are finite; a program needn't handle non-finite values.
Results may differ from a plain program's by a relative error of at most 0.003.
Values may be sent and summed in bfloat16 or wider, within the bound.
A program may use at most 128 MiB of HBM per device.

v0:
```python
import jax
import jax.numpy as jnp
from jax import lax
from jax.sharding import PartitionSpec as P


def local(rhs, factor, inverses):
    count = lax.axis_size("rows")
    place = lax.axis_index("rows")
    cycles, tile, width = rhs.shape
    panels = inverses.shape[0]
    bf16, f32 = jnp.bfloat16, jnp.float32
    tile_ids = jnp.arange(cycles, dtype=jnp.int32) * count + place

    pairs = [(t, p) for t in range(panels) for p in range(t)]
    blocks = jnp.stack([jnp.where(place == t, factor[0, :, p, :], jnp.zeros((), bf16)) for t, p in pairs])
    blocks = lax.all_gather(lax.psum(blocks, "rows"), "rhs", axis=2, tiled=True)
    block_of = {pair: blocks[i] for i, pair in enumerate(pairs)}

    pivots = lax.all_to_all(rhs[0], "rows", split_axis=1, concat_axis=0, tiled=True)
    sent = []
    for t in range(panels):
        pivot = pivots[t * tile:(t + 1) * tile]
        for p in range(t):
            pivot = pivot - jnp.dot(block_of[t, p], sent[p], preferred_element_type=f32)
        solved = jnp.dot(inverses[t], pivot, precision=lax.Precision.HIGHEST)
        sent.append(solved.astype(bf16))
    every = lax.all_gather(jnp.concatenate(sent, axis=0), "rows", axis=0)
    every = jnp.transpose(every, (1, 0, 2)).reshape(panels * tile, width)

    whole = lax.all_gather(factor, "rhs", axis=3, tiled=True)
    seen = tile_ids[:, None] > jnp.arange(panels, dtype=jnp.int32)[None, :]
    whole = jnp.where(seen[:, None, :, None], whole, jnp.zeros((), bf16))
    whole = whole.reshape(cycles, tile, panels * tile)
    state = rhs - jnp.einsum("crk,kn->crn", whole, every, preferred_element_type=f32)
    at = jnp.minimum(place, panels - 1) * tile
    mine = lax.dynamic_slice_in_dim(every, at, tile, axis=0).astype(f32)
    first = jnp.where(place < panels, mine, state[0])
    return jnp.concatenate([first[None], state[1:]], axis=0)


def solution(mesh):
    return jax.shard_map(
        local,
        mesh=mesh,
        in_specs=(P(None, "rows", "rhs"), P(None, "rows", None, "rhs"), P()),
        out_specs=P(None, "rows", "rhs"),
        check_vma=False,
    )
```

profile of v0, /device:TPU:24, one launch (start us, length us, event | category | flops | bytes accessed | tf_op | source)
XLA Modules:
  0.0 411.4 jit_solution(7265404325880932777)
XLA Ops:
  6.5 4.7 %slice.76 = f32[1,512,2048]{2,1,0:T(8,128)} slice(f32[2,512,2048]{2,1,0:T(8,128)} %param.3), slice={[0:1], [0:512], [0:2048]} | slice | bytes 8388608 | tf_op jit(solution)/shard_map/slice | solution.py:20
  11.2 5.4 %copy.39 = f32[1,512,2048]{1,2,0:T(8,128)} copy(f32[1,512,2048]{2,1,0:T(8,128)} %slice.76) | data formatting | bytes 8388608
  16.6 5.3 %copy.28 = f32[512,16,128]{2,0,1:T(8,128)} copy(f32[512,16,128]{0,2,1:T(8,128)} %bitcast.93) | data formatting | bytes 8388608 | tf_op jit(solution)/shard_map/all_to_all | solution.py:20
  21.9 7.1 %all-to-all-start = ((f32[512,16,128]{2,0,1:T(8,128)}), f32[512,16,128]{2,0,1:T(8,128)}, u32[]{:S(2)}, u32[]{:S(2)}) async-start(f32[512,16,128]{2,0,1:T(8,128)} %copy.28), calls=%async_computation | async-start | bytes 8388608 | tf_op jit(solution)/shard_map/all_to_all | solution.py:20
  29.1 0.0 all-reduce.2.cloned.1.call-start
  29.1 0.0 copy-done
  29.1 1.1 fusion.13
  30.2 0.1 bitcast_dynamic-update-slice_fusion.4
  30.3 0.1 bitcast_dynamic-update-slice_fusion.3
  30.4 0.1 bitcast_dynamic-update-slice_fusion.2
  30.4 0.1 bitcast_dynamic-update-slice_fusion.1
  30.5 0.1 bitcast_dynamic-update-slice_fusion
  30.5 0.1 fusion.12
  30.6 0.0 copy-start.3
  30.6 1.2 copy-done.3
  31.8 0.0 all-reduce.2.cloned.1.call-update
  31.8 0.0 all-gather.5.cloned.1.call-start
  31.8 176.6 %all-reduce.2.cloned.1.call-done = bf16[6,512,256]{2,1,0:T(8,128)(2,1)} async-done(((bf16[6,512,256]{2,1,0:T(8,128)(2,1)}), bf16[6,512,256]{2,1,0:T(8,128)(2,1)}) %all-reduce.2.cloned.1.call-update) | async-done | bytes 1572880 | tf_op jit(solution)/shard_map/psum | solution.py:17
  208.5 0.0 all-gather.5.cloned.1.call-update
  208.5 0.0 all-gather.7.cloned.1.call-start
  208.6 0.7 all-gather.7.cloned.1.call-update
  209.2 0.0 all-gather.9.cloned.1.call-start
  209.3 0.0 all-to-all-done
  209.3 2.3 convolution_convert_fusion.3
  211.6 11.2 %all-gather.5.cloned.1.call-done = bf16[6,512,512]{2,1,0:T(8,128)(2,1)} async-done(((bf16[6,512,256]{2,1,0:T(8,128)(2,1)}), bf16[6,512,512]{2,1,0:T(8,128)(2,1)}) %all-gather.5.cloned.1.call-update) | async-done | bytes 3145744 | tf_op jit(solution)/shard_map/all_gather | solution.py:17
  222.7 1.5 convolution_subtract_fusion.6
  224.3 1.4 convolution_subtract_fusion.5
  225.7 1.4 convolution_subtract_fusion.3
  227.1 2.2 convolution_convert_fusion.2
  229.3 1.3 convolution_subtract_fusion.4
  230.7 1.4 convolution_subtract_fusion.2
  232.1 1.0 convolution_convert_fusion.1
  233.1 1.4 convolution_subtract_fusion.1
  234.5 1.0 fusion.2
  235.5 0.9 pad_maximum_fusion.1
  236.4 0.0 all-gather.9.cloned.1.call-update
  236.4 0.1 iota_compare_fusion
  236.5 1.8 all-gather.7.cloned.1.call-done
  238.3 5.9 %broadcast_select_fusion = bf16[2,512,4,512]{3,2,1,0:T(4,128)(2,1)} fusion(bf16[2,512,4,512]{3,2,1,0:T(4,128)(2,1)} %all-gather.7.cloned.1.call-done, pred[2,4]{1,0:T(4,128)(4,1)S(1)} %iota_compare_fusion), kind=kLoop, calls=%fused_computation.5 | loop fusion | flops 2097152 | bytes 8388616 | tf_op jit(solution)/shard_map/jit(_where)/select_n | solution.py:33
  244.2 7.8 %reshape.118 = bf16[2,512,2048]{2,1,0:T(8,128)(2,1)} reshape(bf16[2,512,4,512]{3,2,1,0:T(4,128)(2,1)} %broadcast_select_fusion) | data formatting | bytes 8388608 | tf_op jit(solution)/shard_map/reshape | solution.py:34
  252.0 100.3 %all-gather.9.cloned.1.call-done = bf16[32768,128]{1,0:T(8,128)(2,1)} async-done(((bf16[2048,128]{1,0:T(8,128)(2,1)}), bf16[32768,128]{1,0:T(8,128)(2,1)}) %all-gather.9.cloned.1.call-update) | async-done | bytes 8388624 | tf_op jit(solution)/shard_map/all_gather | solution.py:28
  352.3 10.3 %copy.35 = bf16[2048,16,128]{2,1,0:T(8,128)(2,1)} copy(bf16[2048,16,128]{2,0,1:T(8,128)(2,1)} %bitcast.91) | data formatting | bytes 16777216 | tf_op jit(solution)/shard_map/transpose | solution.py:29
  362.6 13.3 %reshape.120 = bf16[2048,2048,1]{1,0,2:T(8,128)(2,1)} reshape(bf16[2048,16,128]{2,1,0:T(8,128)(2,1)} %copy.35) | data formatting | bytes 16777216 | tf_op jit(solution)/shard_map/reshape | solution.py:29
  376.0 9.3 %copy.55 = bf16[16,256,8,128]{3,2,0,1:T(8,128)(2,1)} copy(bf16[16,256,8,128]{3,2,1,0:T(8,128)(2,1)} %bitcast.92) | data formatting | bytes 16777216 | tf_op jit(solution)/shard_map/reshape | solution.py:29
  385.3 12.6 %convolution_subtract_fusion = f32[2,512,2048]{2,1,0:T(8,128)S(1)} fusion(f32[2,512,2048]{2,1,0:T(8,128)} %param.3, bf16[2,512,2048]{2,1,0:T(8,128)(2,1)S(1)} %copy-done.2, bf16[2048,2048,1]{1,0,2:T(8,128)(2,1)} %reshape.120), kind=kOutput, calls=%fused_computation.6 | convolution fusion | flops 8592031744 | bytes 29360128 | tf_op jit(solution)/shard_map/crk,kn->crn/dot_general | solution.py:35
  397.9 0.5 slice.110
  398.4 2.5 fusion.1
  400.9 4.0 pad_maximum_fusion
  (6 shorter events, 0.0 us)
Async XLA Ops:
  21.9 7.2 %copy-start = (bf16[2,512,4,256]{3,2,1,0:T(4,128)(2,1)S(1)}, bf16[2,512,4,256]{3,2,1,0:T(4,128)(2,1)}, u32[]{:S(2)}) copy-start(bf16[2,512,4,256]{3,2,1,0:T(4,128)(2,1)} %param.4) | copy-start | bytes 6291460
  21.9 187.4 %all-to-all-start = ((f32[512,16,128]{2,0,1:T(8,128)}), f32[512,16,128]{2,0,1:T(8,128)}, u32[]{:S(2)}, u32[]{:S(2)}) async-start(f32[512,16,128]{2,0,1:T(8,128)} %copy.28), calls=%async_computation | async-start | bytes 8388608 | tf_op jit(solution)/shard_map/all_to_all | solution.py:20
  29.1 179.4 %all-reduce.2.cloned.1.call-start = ((), (), s32[]{:S(2)}) async-start(), calls=%async_computation.1 | async-start | bytes 3145728 | tf_op jit(solution)/shard_map/psum | solution.py:17
  30.6 1.2 copy-start.3
  31.8 190.9 %all-gather.5.cloned.1.call-start = ((), (), s32[]{:S(2)}) async-start(), calls=%async_computation.2 | async-start | bytes 4718592 | tf_op jit(solution)/shard_map/all_gather | solution.py:17
  208.5 29.8 %all-gather.7.cloned.1.call-start = ((), (), s32[]{:S(2)}) async-start(), calls=%async_computation.3 | async-start | bytes 6291456 | tf_op jit(solution)/shard_map/all_gather | solution.py:31
  209.2 143.0 %all-gather.9.cloned.1.call-start = ((), (), s32[]{:S(2)}) async-start(), calls=%async_computation.4 | async-start | bytes 8912896 | tf_op jit(solution)/shard_map/all_gather | solution.py:28
  222.7 9.3 %copy-start.1 = (f32[4,512,512]{2,1,0:T(8,128)S(1)}, f32[4,512,512]{2,1,0:T(8,128)}, u32[]{:S(2)}) copy-start(f32[4,512,512]{2,1,0:T(8,128)} %param.5) | copy-start | bytes 12582916
  376.0 9.3 %copy-start.2 = (bf16[2,512,2048]{2,1,0:T(8,128)(2,1)S(1)}, bf16[2,512,2048]{2,1,0:T(8,128)(2,1)}, u32[]{:S(2)}) copy-start(bf16[2,512,2048]{2,1,0:T(8,128)(2,1)} %reshape.118) | copy-start | bytes 12582916
Sparse Core Ops, SparseCore 0:
  35.3 173.1 all-reduce.1
  210.0 12.6 all-gather.4
  224.3 13.9 all-gather.6
  240.9 111.3 all-gather.8
where the time goes:
time: 416 us; the launch traced here: 411 us
  waiting for transfers between devices  291 us (70%)
  local copies, waits for them, and re-layouts  59 us (14%)
  matrix products  27.5 us (7%)
  other arithmetic  13.7 us (3%)
  between operations  13.3 us (3%)
  starting transfers between devices  7.29 us (2%)
    psum x1, waiting for transfers between devices, local(): blocks = lax.all_gather(lax.psum(blocks, 'rows'), 'rhs', axis=2, tiled=True)  177 us
    all_gather x1, waiting for transfers between devices, local(): every = lax.all_gather(jnp.concatenate(sent, axis=0), 'rows', axis=0)  100 us
    reshape x2, local copies, waits for them, and re-layouts, local(): every = jnp.transpose(every, (1, 0, 2)).reshape(panels * tile, width)  22.7 us
    dot_general x1, matrix products, local(): jnp.einsum('crk,kn->crn', whole, every, preferred_element_type=f32)  12.6 us
    all_gather x1, waiting for transfers between devices, local(): blocks = lax.all_gather(lax.psum(blocks, 'rows'), 'rhs', axis=2, tiled=True)  11.2 us
    transpose x1, local copies, waits for them, and re-layouts, local(): every = jnp.transpose(every, (1, 0, 2)).reshape(panels * tile, width)  10.3 us
    dot_general x6, matrix products, local(): pivot = pivot - jnp.dot(block_of[t, p], sent[p], preferred_element_type=f32)  8.5 us
  transfers between devices with their start and end apart: 5, of which 4 were waited for; matrix products, arithmetic and copies ran while one was open for 8% of the time, Pallas kernels for 0%

commit v1 on v0

v1 whole, which is shorter than its diff:
```python
import functools

import jax
import jax.numpy as jnp
from jax import lax
from jax.experimental import pallas as pl
from jax.experimental.pallas import tpu as pltpu
from jax.sharding import PartitionSpec as P

LAGS = ((0, 2, 4, 6), (0, 0, 3, 5), (0, 2, 2, 5), (0, 0, 2, 2))
LANES = 128


def pick(place, values):
    total = jnp.int32(0)
    for i, v in enumerate(values):
        total = total + jnp.where(place == i, jnp.int32(v), jnp.int32(0))
    return total


def kernel(count, rhs, fac, inv, out, sent, fbuf, ibuf, xbuf,
           f_in, f_send, f_recv, i_in, x_in, x_out,
           own_recv, a_recv, b_recv, dx_recv, dy_recv,
           n1_send, n2_send, up_send, ra_send, rb_send):
    chunks, cycles, tile, lanes = xbuf.shape
    panels = inv.shape[0]
    kpart = fac.shape[1] // panels
    half = tile // 2
    planes = count // panels
    bf16, f32 = jnp.bfloat16, jnp.float32

    me = lax.axis_index("rows")
    core = lax.axis_index("rhs")
    z = me // panels
    c = me % panels
    n1 = c + 1 - 2 * (c % 2)
    n2 = (c + 2) % panels
    base = z * panels
    to_core = {"rows": me, "rhs": 1 - core}
    to_n1 = {"rows": base + n1, "rhs": core}
    to_n2 = {"rows": base + n2, "rhs": core}
    to_up = {"rows": jnp.minimum(me + panels, count - 1), "rhs": core}
    to_down = {"rows": jnp.maximum(me - panels, 0), "rhs": core}
    has_up = z < planes - 1
    has_down = z > 0

    def x_load(j):
        cols = pl.ds(pl.multiple_of(j * lanes, lanes), lanes)
        return pltpu.make_async_copy(rhs.at[:, :, cols], xbuf.at[j], x_in.at[j])

    def x_store(j):
        cols = pl.ds(pl.multiple_of(j * lanes, lanes), lanes)
        return pltpu.make_async_copy(xbuf.at[j], out.at[:, :, cols], x_out.at[j])

    def i_load():
        return pltpu.make_async_copy(inv.at[c], ibuf, i_in)

    def f_parts(cycle, p):
        src = fac.at[pl.ds(cycle * tile, tile), pl.ds(p * kpart, kpart)]
        at = pl.multiple_of(p * 2 * kpart + core * kpart, kpart)
        return src, fbuf.at[pl.ds(cycle * tile, tile), pl.ds(at, kpart)], cycle * panels + p

    def f_local(cycle, p):
        src, dst, at = f_parts(cycle, p)
        return pltpu.make_async_copy(src, dst, f_in.at[at])

    def f_remote(cycle, p):
        src, dst, at = f_parts(cycle, p)
        return pltpu.make_async_remote_copy(src, dst, f_send.at[at], f_recv.at[at], device_id=to_core)

    def f_arrive(cycle, p):
        at = pl.multiple_of(p * 2 * kpart + (1 - core) * kpart, kpart)
        dst = fbuf.at[pl.ds(cycle * tile, tile), pl.ds(at, kpart)]
        src, _, s = f_parts(cycle, p)
        return pltpu.make_async_remote_copy(src, dst, f_send.at[s], f_recv.at[s], device_id=to_core)

    def hop(j, p, start, size, send, recv, to):
        at = pl.multiple_of(p * tile + start, half)
        ref = sent.at[j, pl.ds(at, size)]
        return pltpu.make_async_remote_copy(ref, ref, send.at[j], recv.at[j], device_id=to)

    def own_n1(j):
        return hop(j, c, 0, tile, n1_send, a_recv, to_n1)

    def own_n2(j):
        return hop(j, c, 0, tile, n2_send, b_recv, to_n2)

    def own_up(j):
        return hop(j, c, 0, tile, up_send, own_recv, to_up)

    def relay_a(j):
        return hop(j, n1, half, half, ra_send, dy_recv, to_n2)

    def relay_b(j):
        return hop(j, n2, 0, half, rb_send, dx_recv, to_n1)

    def arrive_a(j):
        return hop(j, n1, 0, tile, n1_send, a_recv, to_n1)

    def arrive_b(j):
        return hop(j, n2, 0, tile, n2_send, b_recv, to_n2)

    def arrive_dx(j):
        return hop(j, panels - 1 - c, 0, half, rb_send, dx_recv, to_n1)

    def arrive_dy(j):
        return hop(j, panels - 1 - c, half, half, ra_send, dy_recv, to_n2)

    @pl.when(z == 0)
    def _():
        i_load().start()

    @pl.loop(0, chunks)
    def _(j):
        x_load(j).start()

    for cycle in range(cycles):
        for p in range(panels):
            f_local(cycle, p).start()

    barrier = pltpu.get_barrier_semaphore()
    for to in (to_core, to_n1, to_n2):
        pl.semaphore_signal(barrier, inc=1, device_id=to)

    @pl.when(has_up)
    def _():
        pl.semaphore_signal(barrier, inc=1, device_id=to_up)

    @pl.when(has_down)
    def _():
        pl.semaphore_signal(barrier, inc=1, device_id=to_down)

    pl.semaphore_wait(barrier, 3 + jnp.where(has_up, 1, 0) + jnp.where(has_down, 1, 0))

    for cycle in range(cycles):
        for p in range(panels):
            f_remote(cycle, p).start()

    def f_wait(cycle):
        for p in range(panels):
            f_local(cycle, p).wait()
            f_arrive(cycle, p).wait_recv()

    def solve(p, j):
        x_load(j).wait()

        @pl.when(j == 0)
        def _():
            i_load().wait()
            if p > 0:
                f_wait(0)

        pivot = xbuf[j, 0]
        if p > 0:
            pivot = pivot - jnp.dot(fbuf[:tile, : p * tile], sent[j, : p * tile], preferred_element_type=f32)
        solved = jnp.dot(ibuf[...], pivot, precision=lax.Precision.HIGHEST, preferred_element_type=f32)
        sent[j, p * tile:(p + 1) * tile] = solved.astype(bf16)
        xbuf[j, 0] = solved

    def event(p, j):
        @pl.when(p == c)
        def _():
            @pl.when(z == 0)
            def _():
                solve(p, j)

            @pl.when(z > 0)
            def _():
                own_up(j).wait_recv()

            own_n1(j).start()
            own_n2(j).start()

            @pl.when(has_up)
            def _():
                own_up(j).start()

        @pl.when(p == n1)
        def _():
            arrive_a(j).wait_recv()
            relay_a(j).start()

        @pl.when(p == n2)
        def _():
            arrive_b(j).wait_recv()
            relay_b(j).start()

        @pl.when(p == panels - 1 - c)
        def _():
            arrive_dx(j).wait_recv()
            arrive_dy(j).wait_recv()

    def update(j):
        @pl.when(j == 0)
        def _():
            f_wait(1)

            @pl.when((z > 0) | (c == 0))
            def _():
                f_wait(0)

        @pl.when(z > 0)
        def _():
            x_load(j).wait()

        @pl.loop(jnp.where(z == 0, 1, 0), cycles)
        def _(cycle):
            rows = pl.ds(pl.multiple_of(cycle * tile, tile), tile)
            delta = jnp.dot(fbuf[rows, :], sent[j], preferred_element_type=f32)
            xbuf[j, cycle] = xbuf[j, cycle] - delta

        x_store(j).start()

    lags = [pick(c, [row[p] for row in LAGS]) for p in range(panels)]
    last = max(max(row) for row in LAGS)
    final = lags[0]
    for lag in lags[1:]:
        final = jnp.maximum(final, lag)

    @pl.loop(0, chunks + last)
    def _(r):
        for p in range(panels):
            j = r - lags[p]

            @pl.when((j >= 0) & (j < chunks))
            def _():
                event(p, j)

        done = r - final

        @pl.when((done >= 0) & (done < chunks))
        def _():
            update(done)

    @pl.loop(0, chunks)
    def _(j):
        own_n1(j).wait_send()
        own_n2(j).wait_send()
        relay_a(j).wait_send()
        relay_b(j).wait_send()

        @pl.when(has_up)
        def _():
            own_up(j).wait_send()

        x_store(j).wait()

    for cycle in range(cycles):
        for p in range(panels):
            f_remote(cycle, p).wait_send()


def local(rhs, factor, inverses):
    count = lax.axis_size("rows")
    cycles, tile, width = rhs.shape
    panels = inverses.shape[0]
    kpart = factor.shape[3]
    chunks = width // LANES
    bf16, f32 = jnp.bfloat16, jnp.float32
    fac = factor.reshape(cycles * tile, panels * kpart)
    dma = lambda n: pltpu.SemaphoreType.DMA((n,))
    return pl.pallas_call(
        functools.partial(kernel, count),
        out_shape=jax.ShapeDtypeStruct(rhs.shape, f32),
        in_specs=[pl.BlockSpec(memory_space=pl.ANY)] * 3,
        out_specs=pl.BlockSpec(memory_space=pl.ANY),
        scratch_shapes=[
            pltpu.VMEM((chunks, panels * tile, LANES), bf16),
            pltpu.VMEM((cycles * tile, panels * tile), bf16),
            pltpu.VMEM((tile, tile), f32),
            pltpu.VMEM((chunks, cycles, tile, LANES), f32),
            dma(cycles * panels), dma(cycles * panels), dma(cycles * panels),
            pltpu.SemaphoreType.DMA, dma(chunks), dma(chunks),
            dma(chunks), dma(chunks), dma(chunks), dma(chunks), dma(chunks),
            dma(chunks), dma(chunks), dma(chunks), dma(chunks), dma(chunks),
        ],
        compiler_params=pltpu.CompilerParams(
            collective_id=0, has_side_effects=True, vmem_limit_bytes=56 << 20
        ),
        name="substitute",
    )(rhs, fac, inverses)


def solution(mesh):
    return jax.shard_map(
        local,
        mesh=mesh,
        in_specs=(P(None, "rows", "rhs"), P(None, "rows", None, "rhs"), P()),
        out_specs=P(None, "rows", "rhs"),
        check_vma=False,
    )
```

time: 416 us -> 198 us (0.48); the launches traced: 411 us -> 198 us
  waiting for transfers between devices: 291 us -> 0 us
  Pallas kernels: 0 us -> 187 us
  local copies, waits for them, and re-layouts: 59 us -> 11.3 us
  matrix products: 27.5 us -> 0 us
  other arithmetic: 13.7 us -> 0 us
  between operations: 13.3 us -> 0.01 us
  starting transfers between devices: 7.29 us -> 0 us
    pallas_call x0 -> x1, Pallas kernels: none -> 187 us  [local(): pl.pallas_call(functools.partial(kernel, count), out_shape=jax.ShapeDtype...]
    psum x1 -> x0, waiting for transfers between devices: 177 us -> none  [local(): blocks = lax.all_gather(lax.psum(blocks, 'rows'), 'rhs', axis=2, tiled=True)]
    all_gather x3 -> x0, waiting for transfers between devices: 113 us -> none  [the longest x1 100 us: local(): every = lax.all_gather(jnp.concatenate(sent, axis=0), 'rows', axis=0)]
    reshape x3 -> x0, local copies, waits for them, and re-layouts: 30.5 us -> none  [the longest x2 22.7 us: local(): every = jnp.transpose(every, (1, 0, 2)).reshape(panels * tile, width)]
    dot_general x11 -> x0, matrix products: 27.5 us -> none  [the longest x1 12.6 us: local(): jnp.einsum('crk,kn->crn', whole, every, preferred_element_type=f32)]
    transpose x1 -> x0, local copies, waits for them, and re-layouts: 10.3 us -> none  [local(): every = jnp.transpose(every, (1, 0, 2)).reshape(panels * tile, width)]
    all_to_all x1 -> x0, starting transfers between devices: 7.13 us -> none  [local(): lax.all_to_all(rhs[0], 'rows', split_axis=1, concat_axis=0, tiled=True)]
    slice x3 -> x0, local copies, waits for them, and re-layouts: 6.29 us -> none  [the longest x1 4.7 us: local(): rhs[0]]
  transfers between devices with their start and end apart: 5 -> 0, of which waited for: 4 -> 0; matrix products, arithmetic and copies ran while one was open for 8% -> 0% of each run, Pallas kernels for 0% -> 0%
where the time goes in v1:
time: 198 us
  Pallas kernels  187 us (94%)
  local copies, waits for them, and re-layouts  11.3 us (6%)
    pallas_call x1, Pallas kernels, local(): pl.pallas_call(functools.partial(kernel, count), out_shape=jax.ShapeDtype...  187 us
    unnamed x2, local copies, waits for them, and re-layouts  11.3 us

profile of v1, /device:TPU:24, one launch (start us, length us, event | category | flops | bytes accessed | tf_op | source)
XLA Modules:
  0.0 198.1 jit_solution(4773496454373896340)
XLA Ops:
  0.0 3.4 %copy.4 = bf16[128,8,4,256]{3,1,2,0:T(8,128)(2,1)} copy(bf16[128,8,4,256]{3,2,1,0:T(4,128)(2,1)} %bitcast.4) | data formatting | bytes 4194304
  3.4 186.8 %substitute.1 = f32[2,512,2048]{2,1,0:T(8,128)} custom-call(f32[2,512,2048]{2,1,0:T(8,128)} %rhs.1, bf16[1024,1024]{1,0:T(8,128)(2,1)} %bitcast.3, f32[4,512,512]{2,1,0:T(8,128)} %inv.1), custom_call_target="tpu_custom_call" | custom-call | tf_op jit(solution)/shard_map/substitute/pallas_call | solution.py:262
  190.2 7.9 %copy.6 = f32[2,512,2048]{2,1,0:T(8,128)} copy(f32[2,512,2048]{2,1,0:T(8,128)} %substitute.1) | data formatting | bytes 16777216

commit v2 on v1

--- a/solution.py
+++ b/solution.py
@@ -7,7 +7,8 @@
 from jax.experimental.pallas import tpu as pltpu
 from jax.sharding import PartitionSpec as P
 
-LAGS = ((0, 2, 4, 6), (0, 0, 3, 5), (0, 2, 2, 5), (0, 0, 2, 2))
+LAGS = ((1, 3, 9, 17), (0, 0, 8, 8), (3, 5, 5, 7), (4, 4, 6, 6))
+LAGS_UP = ((7, 10, 13, 17), (1, 1, 9, 9), (5, 8, 6, 9), (3, 3, 4, 4))
 LANES = 128
 
 
@@ -16,6 +17,11 @@
     for i, v in enumerate(values):
         total = total + jnp.where(place == i, jnp.int32(v), jnp.int32(0))
     return total
+
+
+def split(x):
+    high = x.astype(jnp.bfloat16)
+    return high, (x - high.astype(jnp.float32)).astype(jnp.bfloat16)
 
 
 def kernel(count, rhs, fac, inv, out, sent, fbuf, ibuf, xbuf,
@@ -153,7 +159,13 @@
         pivot = xbuf[j, 0]
         if p > 0:
             pivot = pivot - jnp.dot(fbuf[:tile, : p * tile], sent[j, : p * tile], preferred_element_type=f32)
-        solved = jnp.dot(ibuf[...], pivot, precision=lax.Precision.HIGHEST, preferred_element_type=f32)
+        inv_high, inv_low = split(ibuf[...])
+        high, low = split(pivot)
+        solved = (
+            jnp.dot(inv_low, high, preferred_element_type=f32)
+            + jnp.dot(inv_high, low, preferred_element_type=f32)
+            + jnp.dot(inv_high, high, preferred_element_type=f32)
+        )
         sent[j, p * tile:(p + 1) * tile] = solved.astype(bf16)
         xbuf[j, 0] = solved
 
@@ -211,8 +223,11 @@
 
         x_store(j).start()
 
-    lags = [pick(c, [row[p] for row in LAGS]) for p in range(panels)]
-    last = max(max(row) for row in LAGS)
+    lags = [
+        jnp.where(z == 0, pick(c, [row[p] for row in LAGS]), pick(c, [row[p] for row in LAGS_UP]))
+        for p in range(panels)
+    ]
+    last = max(max(row) for row in LAGS + LAGS_UP)
     final = lags[0]
     for lag in lags[1:]:
         final = jnp.maximum(final, lag)

time: 198 us -> 127 us (0.64)
  Pallas kernels: 187 us -> 116 us
    pallas_call x1, Pallas kernels: 187 us -> 116 us  [local(): pl.pallas_call(functools.partial(kernel, count), out_shape=jax.ShapeDtype...]
where the time goes in v2:
time: 127 us
  Pallas kernels  116 us (91%)
  local copies, waits for them, and re-layouts  11.3 us (9%)
    pallas_call x1, Pallas kernels, local(): pl.pallas_call(functools.partial(kernel, count), out_shape=jax.ShapeDtype...  116 us
    unnamed x2, local copies, waits for them, and re-layouts  11.3 us

profile of v2, /device:TPU:24, one launch (start us, length us, event | category | flops | bytes accessed | tf_op | source)
XLA Modules:
  0.0 127.0 jit_solution(16800371830442062425)
XLA Ops:
  0.0 3.4 %copy.4 = bf16[128,8,4,256]{3,1,2,0:T(8,128)(2,1)} copy(bf16[128,8,4,256]{3,2,1,0:T(4,128)(2,1)} %bitcast.4) | data formatting | bytes 4194304
  3.4 115.7 %substitute.1 = f32[2,512,2048]{2,1,0:T(8,128)} custom-call(f32[2,512,2048]{2,1,0:T(8,128)} %rhs.1, bf16[1024,1024]{1,0:T(8,128)(2,1)} %bitcast.3, f32[4,512,512]{2,1,0:T(8,128)} %inv.1), custom_call_target="tpu_custom_call" | custom-call | tf_op jit(solution)/shard_map/substitute/pallas_call | solution.py:277
  119.1 7.9 %copy.6 = f32[2,512,2048]{2,1,0:T(8,128)} copy(f32[2,512,2048]{2,1,0:T(8,128)} %substitute.1) | data formatting | bytes 16777216

commit v3 on v1

v3 whole, which is shorter than its diff:
```python
import functools

import jax
import jax.numpy as jnp
from jax import lax
from jax.experimental import pallas as pl
from jax.experimental.pallas import tpu as pltpu
from jax.sharding import PartitionSpec as P

LANES = 128
PARTS = 2
SHARE = 10
FIRST = (
    (111366568, 152736309, 148181557, 685019561, 105460297, 415839849, 105682125, 105460317, 307013197, 219780934, 321430683, 325391518, 577582161, 596232348, 460437146, 1073741795, 1073741823),
    (891316800, 891316800, 688417344, 13996230, 90452393, 55143112, 896344614, 642602560, 843756056, 306885144, 10760499, 449652057, 323889562, 443132115, 323826970, 1073741795, 1073741823),
    (285474816, 97026606, 136504385, 17576306, 207981457, 287411098, 154240558, 414819186, 776243416, 414782168, 97030424, 297341531, 425865587, 294444241, 460437363, 1073741795, 1073741823),
    (17043520, 774706241, 633709184, 111518336, 772609088, 772609092, 144344706, 18519690, 349451345, 35869392, 438987354, 892143016, 47461460, 170027546, 725969498, 1073741798, 1073741823),
)
ABOVE = (
    (13897024, 138052149, 245400488, 37389378, 36183169, 507544693, 379654725, 824332507, 420008083, 513835946, 270873883, 69842344, 172956312, 455649371, 458335321, 323823834, 1066252059),
    (136532488, 148144693, 891325768, 292246024, 688196939, 271688406, 64270446, 185553416, 474582344, 282374232, 185342098, 308360238, 186291724, 323611224, 592263314, 342468250, 1066247834),
    (270565376, 841030544, 97027141, 152512083, 414781576, 810297537, 809804317, 270931499, 189195907, 436292506, 155292206, 407997338, 319337330, 711280181, 711267022, 514435278, 1066252059),
    (150995520, 774706824, 439125058, 406853966, 285926097, 648386184, 694525954, 648126678, 45626049, 828945472, 892084965, 483763848, 299212800, 474146443, 292084944, 860702067, 1066874069),
)
X_FIRST = (0x2bede654, 0xfffc99d2, 0x15473ff, 0x81389afe)
Y_FIRST = (0xd41219ab, 0x3662d, 0xfeab8c00, 0x7ec76501)
X_ABOVE = (0x40a0586c, 0x5338849b, 0x10a046b8, 0x7c10c41)
Y_ABOVE = (0x20068100, 0x20a24, 0xef4e2044, 0xf8168004)
U_ABOVE = (0x9f592693, 0xacc57140, 0x119903, 0x2873ba)


def pick(place, values):
    total = jnp.int32(0)
    for i, v in enumerate(values):
        total = total + jnp.where(place == i, jnp.int32(v), jnp.int32(0))
    return total


def signed(mask):
    return mask - (1 << 32) if mask >= 1 << 31 else mask


def split(x):
    high = x.astype(jnp.bfloat16)
    return high, (x - high.astype(jnp.float32)).astype(jnp.bfloat16)


def kernel(count, rhs, fac, inv, out, sent, fbuf, ibuf, ihigh, ilow, xbuf,
           f_in, f_send, f_recv, i_in, x_in, x_out,
           own_recv, a_recv, b_recv, d_recv,
           x_send, y_send, up_send, rx_send, ry_send, ru_send):
    chunks, cycles, tile, lanes = xbuf.shape
    panels = inv.shape[0]
    kpart = fac.shape[1] // panels
    size = tile // PARTS
    planes = count // panels
    bf16, f32 = jnp.bfloat16, jnp.float32

    me = lax.axis_index("rows")
    core = lax.axis_index("rhs")
    z = me // panels
    c = me % panels
    n1 = c + 1 - 2 * (c % 2)
    n2 = (c + 2) % panels
    across = panels - 1 - c
    base = z * panels
    to_core = {"rows": me, "rhs": 1 - core}
    to_n1 = {"rows": base + n1, "rhs": core}
    to_n2 = {"rows": base + n2, "rhs": core}
    to_up = {"rows": jnp.minimum(me + panels, count - 1), "rhs": core}
    to_down = {"rows": jnp.maximum(me - panels, 0), "rhs": core}
    solves = z == 0
    has_up = z < planes - 1
    early = solves & (c == 0)

    def table(first, above, place):
        return jnp.where(solves, pick(place, first), pick(place, above))

    x_mask = table([signed(m) for m in X_FIRST], [signed(m) for m in X_ABOVE], n1)
    y_mask = table([signed(m) for m in Y_FIRST], [signed(m) for m in Y_ABOVE], n2)
    u_mask = jnp.where(has_up, pick(c, [signed(m) for m in U_ABOVE]), 0)

    def bit(mask, k):
        return (jnp.right_shift(mask, k) & 1) == 1

    def x_load(j):
        cols = pl.ds(pl.multiple_of(j * lanes, lanes), lanes)
        return pltpu.make_async_copy(rhs.at[:, :, cols], xbuf.at[j], x_in.at[j])

    def x_store(j):
        cols = pl.ds(pl.multiple_of(j * lanes, lanes), lanes)
        return pltpu.make_async_copy(xbuf.at[j], out.at[:, :, cols], x_out.at[j])

    def i_load():
        return pltpu.make_async_copy(inv.at[c], ibuf, i_in)

    def f_parts(cycle, p, half):
        src = fac.at[pl.ds(cycle * tile, tile), pl.ds(p * kpart, kpart)]
        at = pl.multiple_of(p * 2 * kpart + half * kpart, kpart)
        return src, fbuf.at[pl.ds(cycle * tile, tile), pl.ds(at, kpart)], cycle * panels + p

    def f_local(cycle, p):
        src, dst, at = f_parts(cycle, p, core)
        return pltpu.make_async_copy(src, dst, f_in.at[at])

    def f_remote(cycle, p, half):
        src, dst, at = f_parts(cycle, p, half)
        return pltpu.make_async_remote_copy(src, dst, f_send.at[at], f_recv.at[at], device_id=to_core)

    def hop(p, k, send, recv, to):
        at = pl.multiple_of(p * tile + (k % PARTS) * size, size)
        ref = sent.at[k // PARTS, pl.ds(at, size)]
        return pltpu.make_async_remote_copy(ref, ref, send.at[k], recv.at[k], device_id=to)

    own_x = lambda k: hop(c, k, x_send, a_recv, to_n1)
    own_y = lambda k: hop(c, k, y_send, b_recv, to_n2)
    own_up = lambda k: hop(c, k, up_send, own_recv, to_up)
    relay_x = lambda k: hop(n2, k, rx_send, d_recv, to_n1)
    relay_y = lambda k: hop(n1, k, ry_send, d_recv, to_n2)
    relay_up = lambda k: hop(across, k, ru_send, d_recv, to_up)
    arrive_a = lambda k: hop(n1, k, x_send, a_recv, to_n1)
    arrive_b = lambda k: hop(n2, k, y_send, b_recv, to_n2)
    arrive_d = lambda k: hop(across, k, rx_send, d_recv, to_n1)

    barrier = pltpu.get_barrier_semaphore()
    for to in (to_core, to_n1, to_n2):
        pl.semaphore_signal(barrier, inc=1, device_id=to)

    @pl.when(has_up)
    def _():
        pl.semaphore_signal(barrier, inc=1, device_id=to_up)

    @pl.when(z > 0)
    def _():
        pl.semaphore_signal(barrier, inc=1, device_id=to_down)

    @pl.when(solves)
    def _():
        i_load().start()

    x_load(0).start()
    for cycle in range(cycles):
        for p in range(panels):
            f_local(cycle, p).start()

    @pl.loop(1, chunks)
    def _(j):
        x_load(j).start()

    pl.semaphore_wait(barrier, 3 + jnp.where(has_up, 1, 0) + jnp.where(z > 0, 1, 0))

    for cycle in range(cycles):
        for p in range(panels):
            f_remote(cycle, p, core).start()

    def f_wait(cycle):
        for p in range(panels):
            f_local(cycle, p).wait()
            f_remote(cycle, p, 1 - core).wait_recv()

    @pl.when(solves)
    def _():
        i_load().wait()
        high, low = split(ibuf[...])
        ihigh[...] = high
        ilow[...] = low

    @pl.when(jnp.logical_not(early))
    def _():
        @pl.loop(0, chunks)
        def _(j):
            x_load(j).wait()

    @pl.when(solves & (c > 0))
    def _():
        f_wait(0)

    def correct(p, j):
        rows = slice(p * tile, (p + 1) * tile)
        delta = jnp.dot(fbuf[:tile, rows], sent[j, rows], preferred_element_type=f32)
        xbuf[j, 0] = xbuf[j, 0] - delta

    def solve(p, j):
        if p == 0:
            x_load(j).wait()
        high, low = split(xbuf[j, 0])
        both = jnp.concatenate([high, low], axis=1)
        for r in range(PARTS):
            rows = slice(r * size, (r + 1) * size)
            depth = (r + 1) * size
            wide = jnp.dot(ihigh[rows, :depth], both[:depth], preferred_element_type=f32)
            rest = jnp.dot(ilow[rows, :depth], high[:depth], preferred_element_type=f32)
            solved = rest + wide[:, lanes:] + wide[:, :lanes]
            sent[j, p * tile + r * size:p * tile + (r + 1) * size] = solved.astype(bf16)
            xbuf[j, 0, rows] = solved

    def take(p, k):
        @pl.when(p == c)
        def _():
            @pl.when(solves)
            def _():
                solve(p, k // PARTS)
                own_up(k).start()
                own_up(k + 1).start()

            @pl.when(z > 0)
            def _():
                own_up(k).wait_recv()

                @pl.when(has_up)
                def _():
                    own_up(k).start()

        @pl.when(p == n1)
        def _():
            arrive_a(k).wait_recv()

            @pl.when(bit(y_mask, k))
            def _():
                relay_y(k).start()

        @pl.when(p == n2)
        def _():
            arrive_b(k).wait_recv()

            @pl.when(bit(x_mask, k))
            def _():
                relay_x(k).start()

        @pl.when(p == across)
        def _():
            arrive_d(k).wait_recv()

            @pl.when(bit(u_mask, k))
            def _():
                relay_up(k).start()

        @pl.when(solves & (p < c) & (k % PARTS == PARTS - 1))
        def _():
            correct(p, k // PARTS)

    def update(u):
        @pl.when(u == 0)
        def _():
            f_wait(1)

            @pl.when((z > 0) | (c == 0))
            def _():
                f_wait(0)

        @pl.loop(jnp.where(solves, 1, 0), cycles)
        def _(cycle):
            rows = pl.ds(pl.multiple_of(cycle * tile, tile), tile)
            both = jnp.concatenate([sent[2 * u], sent[2 * u + 1]], axis=1)
            delta = jnp.dot(fbuf[rows, :], both, preferred_element_type=f32)
            xbuf[2 * u, cycle] = xbuf[2 * u, cycle] - delta[:, :lanes]
            xbuf[2 * u + 1, cycle] = xbuf[2 * u + 1, cycle] - delta[:, lanes:]

        x_store(2 * u).start()
        x_store(2 * u + 1).start()

    words = [table([row[w] for row in FIRST], [row[w] for row in ABOVE], c) for w in range(len(FIRST[0]))]

    def step(_, state):
        word, at, xs, ys, us = state
        symbol = word & 7

        for p in range(panels):
            @pl.when(symbol == p)
            def _():
                take(p, at[p])

        @pl.when(symbol == 4)
        def _():
            update(us)

        @pl.when(symbol == 5)
        def _():
            own_x(2 * xs).start()
            own_x(2 * xs + 1).start()

        @pl.when(symbol == 6)
        def _():
            own_y(2 * ys).start()
            own_y(2 * ys + 1).start()

        at = tuple(
            a + jnp.where(symbol == p, jnp.where(solves & (c == p), PARTS, 1), 0) for p, a in enumerate(at)
        )
        xs = xs + jnp.where(symbol == 5, 1, 0)
        ys = ys + jnp.where(symbol == 6, 1, 0)
        us = us + jnp.where(symbol == 4, 1, 0)
        return jnp.right_shift(word, 3), at, xs, ys, us

    def stride(w, state):
        word = pick(w, [0] * 0)
        for i, value in enumerate(words):
            word = word + jnp.where(w == i, value, 0)
        return lax.fori_loop(0, SHARE, step, (word,) + state)[1:]

    zero = jnp.int32(0)
    lax.fori_loop(0, len(words), stride, ((zero,) * panels, zero, zero, zero))

    @pl.loop(0, chunks * PARTS)
    def _(k):
        own_x(k).wait_send()
        own_y(k).wait_send()

        @pl.when(has_up)
        def _():
            own_up(k).wait_send()

        @pl.when(bit(x_mask, k))
        def _():
            relay_x(k).wait_send()

        @pl.when(bit(y_mask, k))
        def _():
            relay_y(k).wait_send()

        @pl.when(bit(u_mask, k))
        def _():
            relay_up(k).wait_send()

    @pl.loop(0, chunks)
    def _(j):
        x_store(j).wait()

    for cycle in range(cycles):
        for p in range(panels):
            f_remote(cycle, p, core).wait_send()


def local(rhs, factor, inverses):
    count = lax.axis_size("rows")
    cycles, tile, width = rhs.shape
    panels = inverses.shape[0]
    kpart = factor.shape[3]
    chunks = width // LANES
    units = chunks * PARTS
    bf16, f32 = jnp.bfloat16, jnp.float32
    fac = factor.reshape(cycles * tile, panels * kpart)
    dma = lambda n: pltpu.SemaphoreType.DMA((n,))
    return pl.pallas_call(
        functools.partial(kernel, count),
        out_shape=jax.ShapeDtypeStruct(rhs.shape, f32),
        in_specs=[pl.BlockSpec(memory_space=pl.ANY)] * 3,
        out_specs=pl.BlockSpec(memory_space=pl.ANY),
        scratch_shapes=[
            pltpu.VMEM((chunks, panels * tile, LANES), bf16),
            pltpu.VMEM((cycles * tile, panels * tile), bf16),
            pltpu.VMEM((tile, tile), f32),
            pltpu.VMEM((tile, tile), bf16),
            pltpu.VMEM((tile, tile), bf16),
            pltpu.VMEM((chunks, cycles, tile, LANES), f32),
            dma(cycles * panels), dma(cycles * panels), dma(cycles * panels),
            pltpu.SemaphoreType.DMA, dma(chunks), dma(chunks),
        ] + [dma(units)] * 10,
        compiler_params=pltpu.CompilerParams(
            collective_id=0, has_side_effects=True, vmem_limit_bytes=56 << 20
        ),
        name="substitute",
    )(rhs, fac, inverses)


def solution(mesh):
    return jax.shard_map(
        local,
        mesh=mesh,
        in_specs=(P(None, "rows", "rhs"), P(None, "rows", None, "rhs"), P()),
        out_specs=P(None, "rows", "rhs"),
        check_vma=False,
    )
```

time: 198 us -> 119 us (0.60)
  Pallas kernels: 187 us -> 108 us
    pallas_call x1, Pallas kernels: 187 us -> 108 us  [local(): pl.pallas_call(functools.partial(kernel, count), out_shape=jax.ShapeDtype...]
where the time goes in v3:
time: 119 us
  Pallas kernels  108 us (91%)
  local copies, waits for them, and re-layouts  11.3 us (9%)
    pallas_call x1, Pallas kernels, local(): pl.pallas_call(functools.partial(kernel, count), out_shape=jax.ShapeDtype...  108 us
    unnamed x2, local copies, waits for them, and re-layouts  11.3 us

profile of v3, /device:TPU:24, one launch (start us, length us, event | category | flops | bytes accessed | tf_op | source)
XLA Modules:
  0.0 119.2 jit_solution(16196493873833242560)
XLA Ops:
  0.0 3.4 %copy.4 = bf16[128,8,4,256]{3,1,2,0:T(8,128)(2,1)} copy(bf16[128,8,4,256]{3,2,1,0:T(4,128)(2,1)} %bitcast.4) | data formatting | bytes 4194304
  3.4 107.9 %substitute.1 = f32[2,512,2048]{2,1,0:T(8,128)} custom-call(f32[2,512,2048]{2,1,0:T(8,128)} %rhs.1, bf16[1024,1024]{1,0:T(8,128)(2,1)} %bitcast.3, f32[4,512,512]{2,1,0:T(8,128)} %inv.1), custom_call_target="tpu_custom_call" | custom-call | tf_op jit(solution)/shard_map/substitute/pallas_call | solution.py:344
  111.3 7.9 %copy.6 = f32[2,512,2048]{2,1,0:T(8,128)} copy(f32[2,512,2048]{2,1,0:T(8,128)} %substitute.1) | data formatting | bytes 16777216

commit v4 on v3

--- a/solution.py
+++ b/solution.py
@@ -45,8 +45,8 @@
     return high, (x - high.astype(jnp.float32)).astype(jnp.bfloat16)
 
 
-def kernel(count, rhs, fac, inv, out, sent, fbuf, ibuf, ihigh, ilow, xbuf,
-           f_in, f_send, f_recv, i_in, x_in, x_out,
+def kernel(count, rhs, fac, inv, xbuf, sent, fbuf, ibuf, ihigh, ilow,
+           f_in, f_send, f_recv, i_in, x_in,
            own_recv, a_recv, b_recv, d_recv,
            x_send, y_send, up_send, rx_send, ry_send, ru_send):
     chunks, cycles, tile, lanes = xbuf.shape
@@ -87,10 +87,6 @@
         cols = pl.ds(pl.multiple_of(j * lanes, lanes), lanes)
         return pltpu.make_async_copy(rhs.at[:, :, cols], xbuf.at[j], x_in.at[j])
 
-    def x_store(j):
-        cols = pl.ds(pl.multiple_of(j * lanes, lanes), lanes)
-        return pltpu.make_async_copy(xbuf.at[j], out.at[:, :, cols], x_out.at[j])
-
     def i_load():
         return pltpu.make_async_copy(inv.at[c], ibuf, i_in)
 
@@ -256,9 +252,6 @@
             xbuf[2 * u, cycle] = xbuf[2 * u, cycle] - delta[:, :lanes]
             xbuf[2 * u + 1, cycle] = xbuf[2 * u + 1, cycle] - delta[:, lanes:]
 
-        x_store(2 * u).start()
-        x_store(2 * u + 1).start()
-
     words = [table([row[w] for row in FIRST], [row[w] for row in ABOVE], c) for w in range(len(FIRST[0]))]
 
     def step(_, state):
@@ -322,13 +315,25 @@
         def _():
             relay_up(k).wait_send()
 
+    for cycle in range(cycles):
+        for p in range(panels):
+            f_remote(cycle, p, core).wait_send()
+
+
+def place_out(xbuf, out, sems):
+    chunks, _, _, lanes = xbuf.shape
+
+    def store(j):
+        cols = pl.ds(pl.multiple_of(j * lanes, lanes), lanes)
+        return pltpu.make_async_copy(xbuf.at[j], out.at[:, :, cols], sems.at[j])
+
     @pl.loop(0, chunks)
     def _(j):
-        x_store(j).wait()
-
-    for cycle in range(cycles):
-        for p in range(panels):
-            f_remote(cycle, p, core).wait_send()
+        store(j).start()
+
+    @pl.loop(0, chunks)
+    def _(j):
+        store(j).wait()
 
 
 def local(rhs, factor, inverses):
@@ -341,26 +346,34 @@
     bf16, f32 = jnp.bfloat16, jnp.float32
     fac = factor.reshape(cycles * tile, panels * kpart)
     dma = lambda n: pltpu.SemaphoreType.DMA((n,))
-    return pl.pallas_call(
+    state = pl.pallas_call(
         functools.partial(kernel, count),
-        out_shape=jax.ShapeDtypeStruct(rhs.shape, f32),
+        out_shape=pltpu.VMEM((chunks, cycles, tile, LANES), f32),
         in_specs=[pl.BlockSpec(memory_space=pl.ANY)] * 3,
-        out_specs=pl.BlockSpec(memory_space=pl.ANY),
+        out_specs=pl.BlockSpec(memory_space=pltpu.VMEM),
         scratch_shapes=[
             pltpu.VMEM((chunks, panels * tile, LANES), bf16),
             pltpu.VMEM((cycles * tile, panels * tile), bf16),
             pltpu.VMEM((tile, tile), f32),
             pltpu.VMEM((tile, tile), bf16),
             pltpu.VMEM((tile, tile), bf16),
-            pltpu.VMEM((chunks, cycles, tile, LANES), f32),
             dma(cycles * panels), dma(cycles * panels), dma(cycles * panels),
-            pltpu.SemaphoreType.DMA, dma(chunks), dma(chunks),
+            pltpu.SemaphoreType.DMA, dma(chunks),
         ] + [dma(units)] * 10,
         compiler_params=pltpu.CompilerParams(
-            collective_id=0, has_side_effects=True, vmem_limit_bytes=56 << 20
+            collective_id=0, has_side_effects=True, vmem_limit_bytes=40 << 20
         ),
         name="substitute",
     )(rhs, fac, inverses)
+    return pl.pallas_call(
+        place_out,
+        out_shape=jax.ShapeDtypeStruct(rhs.shape, f32),
+        in_specs=[pl.BlockSpec(memory_space=pltpu.VMEM)],
+        out_specs=pl.BlockSpec(memory_space=pl.ANY),
+        scratch_shapes=[dma(chunks)],
+        compiler_params=pltpu.CompilerParams(vmem_limit_bytes=16 << 20),
+        name="place_out",
+    )(state)
 
 
 def solution(mesh):

time: 119 us -> 113 us (0.950)
  local copies, waits for them, and re-layouts: 11.3 us -> 2.08 us
  Pallas kernels: 108 us -> 111 us
    unnamed x2 -> x1, local copies, waits for them, and re-layouts: 11.3 us -> 2.08 us
    pallas_call x1 -> x2, Pallas kernels: 108 us -> 111 us  [the longest x1 108 us: local(): pl.pallas_call(functools.partial(kernel, count), out_shape=pltpu.VMEM((ch...]
where the time goes in v4:
time: 113 us
  Pallas kernels  111 us (98%)
  local copies, waits for them, and re-layouts  2.08 us (2%)
    pallas_call x1, Pallas kernels, local(): pl.pallas_call(functools.partial(kernel, count), out_shape=pltpu.VMEM((ch...  108 us
    pallas_call x1, Pallas kernels, local(): pl.pallas_call(place_out, out_shape=jax.ShapeDtypeStruct(rhs.shape, f32),...  3.42 us

profile of v4, /device:TPU:24, one launch (start us, length us, event | category | flops | bytes accessed | tf_op | source)
XLA Modules:
  0.0 113.2 jit_solution(17939174491828857692)
XLA Ops:
  0.0 2.1 %copy.4 = bf16[128,8,4,256]{3,1,2,0:T(8,128)(2,1)S(1)} copy(bf16[128,8,4,256]{3,2,1,0:T(4,128)(2,1)} %bitcast.4) | data formatting | bytes 4194304
  2.1 107.7 %substitute.1.xbuf = f32[16,2,512,128]{3,2,1,0:T(8,128)S(1)} custom-call(f32[2,512,2048]{2,1,0:T(8,128)} %rhs.1, bf16[1024,1024]{1,0:T(8,128)(2,1)S(1)} %bitcast.3, f32[4,512,512]{2,1,0:T(8,128)} %inv.1), custom_call_target="tpu_custom_call" | custom-call | tf_op jit(solution)/shard_map/substitute/pallas_call | solution.py:349
  109.8 3.4 %place_out.1 = f32[2,512,2048]{2,1,0:T(8,128)} custom-call(f32[16,2,512,128]{3,2,1,0:T(8,128)S(1)} %substitute.1.xbuf), custom_call_target="tpu_custom_call" | custom-call | tf_op jit(solution)/shard_map/place_out/pallas_call | solution.py:368

commit v5 on v4

v5 whole, which is shorter than its diff:
```python
import functools

import jax
import jax.numpy as jnp
from jax import lax
from jax.experimental import pallas as pl
from jax.experimental.pallas import tpu as pltpu
from jax.sharding import PartitionSpec as P

LANES = 128
PARTS = 2
SHARE = 10
FIRST = (
    (111366568, 690180661, 689478214, 306485809, 219730482, 304427673, 689543878, 843889201, 415863912, 289743581, 443328081, 308614302, 577845404, 311277202, 460441307, 1073741795, 1073741823),
    (891316800, 891316800, 891316800, 723544640, 307925190, 81105090, 323697219, 416579866, 891316936, 379859154, 488736531, 327788182, 324089043, 323827859, 443131155, 1073741795, 1073741823),
    (136314880, 809769858, 145171013, 157387650, 143405426, 288218248, 97030702, 140609731, 97026930, 407147291, 187460277, 439143770, 601167477, 893752856, 460437219, 1073741795, 1073741823),
    (17043520, 407179329, 721986101, 856203366, 778376261, 423690308, 36209205, 858270067, 79266901, 5714570, 36330698, 895812979, 47547476, 36334282, 725946795, 1073741798, 1073741823),
)
ABOVE = (
    (13897024, 17256501, 30675061, 352591169, 245896206, 168251472, 174431568, 74403906, 35724610, 40416373, 286372776, 292350481, 342176401, 290559699, 441001179, 457848540, 1066252059),
    (136532488, 148144693, 891325768, 136532488, 315916853, 320509451, 892082328, 276467800, 4595922, 688687017, 306309710, 64259683, 444240579, 309404882, 575485666, 476685971, 1065985746),
    (18874368, 841505922, 776012365, 845230152, 341914181, 407638952, 845222770, 270833861, 273443480, 424415790, 54715092, 177019634, 189108592, 860989298, 153543893, 499992217, 1066252059),
    (136348160, 189010440, 54533466, 438652250, 436493505, 170024144, 97289808, 856265810, 231543013, 3335706, 97322632, 194458714, 2972881, 175184794, 859939187, 778385549, 1066067610),
)
X_FIRST = (0xf77f124, 0xdf7fdd71, 0x1e5eef, 0x820ceafe)
Y_FIRST = (0xf0880edb, 0x2080228e, 0xffe1a110, 0x7df31501)
X_ABOVE = (0x18e64004, 0xee9b4821, 0x88868a1, 0x23043300)
Y_ABOVE = (0x2008289, 0x542, 0xb672120c, 0xdc78cc00)
U_ABOVE = (0xe5193d72, 0x1164b29c, 0x41058552, 0x8300ff)


def pick(place, values):
    total = jnp.int32(0)
    for i, v in enumerate(values):
        total = total + jnp.where(place == i, jnp.int32(v), jnp.int32(0))
    return total


def signed(mask):
    return mask - (1 << 32) if mask >= 1 << 31 else mask


def split(x):
    high = x.astype(jnp.bfloat16)
    return high, (x - high.astype(jnp.float32)).astype(jnp.bfloat16)


def kernel(count, rhs, fac, inv, xbuf, sent, fbuf, fraw, ibuf, ihigh, ilow,
           f_in, f_send, f_recv, i_in, x_in,
           own_recv, a_recv, b_recv, d_recv,
           x_send, y_send, next_send, prev_send, rx_send, ry_send, rn_send, rp_send):
    chunks, cycles, tile, lanes = xbuf.shape
    panels = inv.shape[0]
    kpart = fac.shape[3]
    size = tile // PARTS
    planes = count // panels
    bf16, f32 = jnp.bfloat16, jnp.float32

    me = lax.axis_index("rows")
    core = lax.axis_index("rhs")
    z = me // panels
    c = me % panels
    n1 = c + 1 - 2 * (c % 2)
    n2 = (c + 2) % panels
    across = panels - 1 - c
    base = z * panels
    to_core = {"rows": me, "rhs": 1 - core}
    to_n1 = {"rows": base + n1, "rhs": core}
    to_n2 = {"rows": base + n2, "rhs": core}
    middle = planes // 2
    solves = z == 0
    source = jnp.where(z == middle, 0, jnp.where(z < middle, z + 1, z - 1))
    to_next = ((z == 0) & (planes > 1)) | ((z >= middle) & (z > 0) & (z < planes - 1))
    to_prev = (z <= middle) & (z > 1)
    next_plane = jnp.where(z == 0, middle, jnp.minimum(z + 1, planes - 1))
    at_next = {"rows": next_plane * panels + c, "rhs": core}
    at_prev = {"rows": jnp.maximum(z - 1, 0) * panels + c, "rhs": core}
    at_source = {"rows": source * panels + c, "rhs": core}
    early = solves & (c == 0)

    def table(first, above, place):
        return jnp.where(solves, pick(place, first), pick(place, above))

    x_mask = table([signed(m) for m in X_FIRST], [signed(m) for m in X_ABOVE], n1)
    y_mask = table([signed(m) for m in Y_FIRST], [signed(m) for m in Y_ABOVE], n2)
    u_mask = jnp.where(to_next | to_prev, pick(c, [signed(m) for m in U_ABOVE]), 0)

    def bit(mask, k):
        return (jnp.right_shift(mask, k % 32) & 1) == 1

    def x_load(j):
        cols = pl.ds(pl.multiple_of(j * lanes, lanes), lanes)
        return pltpu.make_async_copy(rhs.at[:, :, cols], xbuf.at[j], x_in.at[j])

    def i_load():
        return pltpu.make_async_copy(inv.at[c], ibuf, i_in)

    def f_load(cycle):
        return pltpu.make_async_copy(fac.at[cycle], fraw.at[cycle], f_in.at[cycle])

    def f_remote(cycle, p, half):
        at = pl.multiple_of(p * 2 * kpart + half * kpart, kpart)
        ref = fbuf.at[pl.ds(cycle * tile, tile), pl.ds(at, kpart)]
        s = cycle * panels + p
        return pltpu.make_async_remote_copy(ref, ref, f_send.at[s], f_recv.at[s], device_id=to_core)

    def f_place(cycle):
        f_load(cycle).wait()
        step = 64

        @pl.loop(0, tile // step)
        def _(i):
            rows = pl.ds(pl.multiple_of(i * step, step), step)
            to = pl.ds(pl.multiple_of(cycle * tile + i * step, step), step)
            block = jnp.transpose(fraw[cycle, rows], (1, 0, 2))
            for p in range(panels):
                at = pl.multiple_of(p * 2 * kpart + core * kpart, kpart)
                fbuf[to, pl.ds(at, kpart)] = block[p]

    def f_share(cycle):
        for p in range(panels):
            f_remote(cycle, p, core).start()

    def hop(p, k, send, recv, to):
        at = pl.multiple_of(p * tile + (k % PARTS) * size, size)
        ref = sent.at[k // PARTS, pl.ds(at, size)]
        return pltpu.make_async_remote_copy(ref, ref, send.at[k], recv.at[k], device_id=to)

    own_x = lambda k: hop(c, k, x_send, a_recv, to_n1)
    own_y = lambda k: hop(c, k, y_send, b_recv, to_n2)
    own_next = lambda k: hop(c, k, next_send, own_recv, at_next)
    own_prev = lambda k: hop(c, k, prev_send, own_recv, at_prev)
    relay_x = lambda k: hop(n2, k, rx_send, d_recv, to_n1)
    relay_y = lambda k: hop(n1, k, ry_send, d_recv, to_n2)
    relay_next = lambda k: hop(across, k, rn_send, d_recv, at_next)
    relay_prev = lambda k: hop(across, k, rp_send, d_recv, at_prev)
    arrive_a = lambda k: hop(n1, k, x_send, a_recv, to_n1)
    arrive_b = lambda k: hop(n2, k, y_send, b_recv, to_n2)
    arrive_d = lambda k: hop(across, k, rx_send, d_recv, to_n1)

    barrier = pltpu.get_barrier_semaphore()
    for to in (to_core, to_n1, to_n2):
        pl.semaphore_signal(barrier, inc=1, device_id=to)

    for on, to in ((to_next, at_next), (to_prev, at_prev), (z > 0, at_source)):
        @pl.when(on)
        def _():
            pl.semaphore_signal(barrier, inc=1, device_id=to)

    @pl.when(solves)
    def _():
        i_load().start()

    x_load(0).start()
    for cycle in range(cycles):
        f_load(cycle).start()

    @pl.loop(1, chunks)
    def _(j):
        x_load(j).start()

    def f_wait(cycle):
        for p in range(panels):
            f_remote(cycle, p, 1 - core).wait_recv()

    @pl.when(solves)
    def _():
        i_load().wait()
        high, low = split(ibuf[...])
        ihigh[...] = high
        ilow[...] = low

    def correct(p, j):
        rows = slice(p * tile, (p + 1) * tile)
        delta = jnp.dot(fbuf[:tile, rows], sent[j, rows], preferred_element_type=f32)
        xbuf[j, 0] = xbuf[j, 0] - delta

    def solve(p, j):
        if p == 0:
            x_load(j).wait()
        high, low = split(xbuf[j, 0])
        both = jnp.concatenate([high, low], axis=1)
        block = tile // 2
        for r in range(2):
            rows = slice(r * block, (r + 1) * block)
            depth = (r + 1) * block
            wide = jnp.dot(ihigh[rows, :depth], both[:depth], preferred_element_type=f32)
            rest = jnp.dot(ilow[rows, :depth], high[:depth], preferred_element_type=f32)
            solved = rest + wide[:, lanes:] + wide[:, :lanes]
            sent[j, p * tile + r * block:p * tile + (r + 1) * block] = solved.astype(bf16)
            xbuf[j, 0, rows] = solved

    @pl.when(early)
    def _():
        solve(0, 0)

    @pl.when(jnp.logical_not(early))
    def _():
        for cycle in range(cycles):
            f_place(cycle)

    words = [table([row[w] for row in FIRST], [row[w] for row in ABOVE], c) for w in range(len(FIRST[0]))]
    pl.semaphore_wait(
        barrier, 3 + jnp.where(to_next, 1, 0) + jnp.where(to_prev, 1, 0) + jnp.where(z > 0, 1, 0)
    )

    @pl.when(jnp.logical_not(early))
    def _():
        for cycle in range(cycles):
            f_share(cycle)

        @pl.loop(0, chunks)
        def _(j):
            x_load(j).wait()

    @pl.when(solves & (c > 0))
    def _():
        f_wait(0)

    def take(p, k):
        @pl.when(p == c)
        def _():
            @pl.when(solves)
            def _():
                if p == 0:
                    @pl.when(k > 0)
                    def _():
                        solve(p, k // PARTS)
                else:
                    solve(p, k // PARTS)

                @pl.when(to_next)
                def _():
                    for i in range(PARTS):
                        own_next(k + i).start()

                if p == 0:
                    @pl.when(k == 3 * PARTS)
                    def _():
                        for cycle in range(cycles):
                            f_place(cycle)
                        for cycle in range(cycles):
                            f_share(cycle)

            @pl.when(z > 0)
            def _():
                own_next(k).wait_recv()

                @pl.when(to_next)
                def _():
                    own_next(k).start()

                @pl.when(to_prev)
                def _():
                    own_prev(k).start()

        @pl.when(p == n1)
        def _():
            arrive_a(k).wait_recv()

            @pl.when(bit(y_mask, k))
            def _():
                relay_y(k).start()

        @pl.when(p == n2)
        def _():
            arrive_b(k).wait_recv()

            @pl.when(bit(x_mask, k))
            def _():
                relay_x(k).start()

        @pl.when(p == across)
        def _():
            arrive_d(k).wait_recv()

            @pl.when(bit(u_mask, k) & to_next)
            def _():
                relay_next(k).start()

            @pl.when(bit(u_mask, k) & to_prev)
            def _():
                relay_prev(k).start()

        @pl.when(solves & (p < c) & (k % PARTS == PARTS - 1))
        def _():
            correct(p, k // PARTS)

    def update(u):
        @pl.when(u == 0)
        def _():
            f_wait(1)

            @pl.when((z > 0) | (c == 0))
            def _():
                f_wait(0)

        @pl.loop(jnp.where(solves, 1, 0), cycles)
        def _(cycle):
            rows = pl.ds(pl.multiple_of(cycle * tile, tile), tile)
            both = jnp.concatenate([sent[2 * u], sent[2 * u + 1]], axis=1)
            delta = jnp.dot(fbuf[rows, :], both, preferred_element_type=f32)
            xbuf[2 * u, cycle] = xbuf[2 * u, cycle] - delta[:, :lanes]
            xbuf[2 * u + 1, cycle] = xbuf[2 * u + 1, cycle] - delta[:, lanes:]

    def step(_, state):
        word, at, xs, ys, us = state
        symbol = word & 7

        for p in range(panels):
            @pl.when(symbol == p)
            def _():
                take(p, at[p])

        @pl.when(symbol == 4)
        def _():
            update(us)

        @pl.when(symbol == 5)
        def _():
            for i in range(PARTS):
                own_x(PARTS * xs + i).start()

        @pl.when(symbol == 6)
        def _():
            for i in range(PARTS):
                own_y(PARTS * ys + i).start()

        at = tuple(
            a + jnp.where(symbol == p, jnp.where(solves & (c == p), PARTS, 1), 0) for p, a in enumerate(at)
        )
        xs = xs + jnp.where(symbol == 5, 1, 0)
        ys = ys + jnp.where(symbol == 6, 1, 0)
        us = us + jnp.where(symbol == 4, 1, 0)
        return jnp.right_shift(word, 3), at, xs, ys, us

    def stride(w, state):
        word = pick(w, [0] * 0)
        for i, value in enumerate(words):
            word = word + jnp.where(w == i, value, 0)
        return lax.fori_loop(0, SHARE, step, (word,) + state)[1:]

    zero = jnp.int32(0)
    lax.fori_loop(0, len(words), stride, ((zero,) * panels, zero, zero, zero))

    @pl.loop(0, chunks * PARTS)
    def _(k):
        own_x(k).wait_send()
        own_y(k).wait_send()

        @pl.when(to_next)
        def _():
            own_next(k).wait_send()

        @pl.when(to_prev)
        def _():
            own_prev(k).wait_send()

        @pl.when(bit(x_mask, k))
        def _():
            relay_x(k).wait_send()

        @pl.when(bit(y_mask, k))
        def _():
            relay_y(k).wait_send()

        @pl.when(bit(u_mask, k) & to_next)
        def _():
            relay_next(k).wait_send()

        @pl.when(bit(u_mask, k) & to_prev)
        def _():
            relay_prev(k).wait_send()

    for cycle in range(cycles):
        for p in range(panels):
            f_remote(cycle, p, core).wait_send()


def place_out(xbuf, out, sems):
    chunks, _, _, lanes = xbuf.shape

    def store(j):
        cols = pl.ds(pl.multiple_of(j * lanes, lanes), lanes)
        return pltpu.make_async_copy(xbuf.at[j], out.at[:, :, cols], sems.at[j])

    @pl.loop(0, chunks)
    def _(j):
        store(j).start()

    @pl.loop(0, chunks)
    def _(j):
        store(j).wait()


def local(rhs, factor, inverses):
    count = lax.axis_size("rows")
    cycles, tile, width = rhs.shape
    panels = inverses.shape[0]
    kpart = factor.shape[3]
    chunks = width // LANES
    units = chunks * PARTS
    bf16, f32 = jnp.bfloat16, jnp.float32
    dma = lambda n: pltpu.SemaphoreType.DMA((n,))
    state = pl.pallas_call(
        functools.partial(kernel, count),
        out_shape=pltpu.VMEM((chunks, cycles, tile, LANES), f32),
        in_specs=[pl.BlockSpec(memory_space=pltpu.HBM)] * 3,
        out_specs=pl.BlockSpec(memory_space=pltpu.VMEM),
        scratch_shapes=[
            pltpu.VMEM((chunks, panels * tile, LANES), bf16),
            pltpu.VMEM((cycles * tile, panels * tile), bf16),
            pltpu.VMEM(factor.shape, bf16),
            pltpu.VMEM((tile, tile), f32),
            pltpu.VMEM((tile, tile), bf16),
            pltpu.VMEM((tile, tile), bf16),
            dma(cycles), dma(cycles * panels), dma(cycles * panels),
            pltpu.SemaphoreType.DMA, dma(chunks),
        ] + [dma(units)] * 12,
        compiler_params=pltpu.CompilerParams(
            collective_id=0, has_side_effects=True, vmem_limit_bytes=55 << 20
        ),
        name="substitute",
    )(rhs, factor, inverses)
    return pl.pallas_call(
        place_out,
        out_shape=jax.ShapeDtypeStruct(rhs.shape, f32),
        in_specs=[pl.BlockSpec(memory_space=pltpu.VMEM)],
        out_specs=pl.BlockSpec(memory_space=pl.ANY),
        scratch_shapes=[dma(chunks)],
        compiler_params=pltpu.CompilerParams(vmem_limit_bytes=16 << 20),
        name="place_out",
    )(state)


def solution(mesh):
    return jax.shard_map(
        local,
        mesh=mesh,
        in_specs=(P(None, "rows", "rhs"), P(None, "rows", None, "rhs"), P()),
        out_specs=P(None, "rows", "rhs"),
        check_vma=False,
    )
```

time: 113 us -> 103 us (0.912); the launches traced: 113 us -> 102 us
  Pallas kernels: 111 us -> 102 us
  local copies, waits for them, and re-layouts: 2.08 us -> 0 us
    pallas_call x1, Pallas kernels: 108 us -> 98.6 us  [local(): pl.pallas_call(functools.partial(kernel, count), out_shape=pltpu.VMEM((ch...]
    unnamed x1 -> x0, local copies, waits for them, and re-layouts: 2.08 us -> none
where the time goes in v5:
time: 103 us; the launch traced here: 102 us
  Pallas kernels  102 us (99%)
    pallas_call x1, Pallas kernels, local(): pl.pallas_call(functools.partial(kernel, count), out_shape=pltpu.VMEM((ch...  98.6 us
    pallas_call x1, Pallas kernels, local(): pl.pallas_call(place_out, out_shape=jax.ShapeDtypeStruct(rhs.shape, f32),...  3.42 us

profile of v5, /device:TPU:24, one launch (start us, length us, event | category | flops | bytes accessed | tf_op | source)
XLA Modules:
  0.0 102.0 jit_solution(1312527509075810250)
XLA Ops:
  0.0 98.6 %substitute.1.xbuf = f32[16,2,512,128]{3,2,1,0:T(8,128)S(1)} custom-call(f32[2,512,2048]{2,1,0:T(8,128)} %rhs.1, bf16[2,512,4,256]{3,2,1,0:T(4,128)(2,1)} %fac.1, f32[4,512,512]{2,1,0:T(8,128)} %inv.1), custom_call_target="tpu_custom_call" | custom-call | tf_op jit(solution)/shard_map/substitute/pallas_call | solution.py:405
  98.6 3.4 %place_out.1 = f32[2,512,2048]{2,1,0:T(8,128)} custom-call(f32[16,2,512,128]{3,2,1,0:T(8,128)S(1)} %substitute.1.xbuf), custom_call_target="tpu_custom_call" | custom-call | tf_op jit(solution)/shard_map/place_out/pallas_call | solution.py:425

commit v6 on v5

--- a/solution.py
+++ b/solution.py
@@ -312,7 +312,7 @@
             def _():
                 take(p, at[p])
 
-        @pl.when(symbol == 4)
+        @pl.when((symbol == 4) & (us < chunks // 2 - 1))
         def _():
             update(us)
 
@@ -377,20 +377,38 @@
             f_remote(cycle, p, core).wait_send()
 
 
-def place_out(xbuf, out, sems):
-    chunks, _, _, lanes = xbuf.shape
-
-    def store(j):
+def finish(panels, xbuf, sent, fbuf, out, last, sems):
+    chunks, cycles, tile, lanes = xbuf.shape
+    first = chunks - 2
+    solves = lax.axis_index("rows") < panels
+
+    def store(j, ref):
         cols = pl.ds(pl.multiple_of(j * lanes, lanes), lanes)
-        return pltpu.make_async_copy(xbuf.at[j], out.at[:, :, cols], sems.at[j])
+        return pltpu.make_async_copy(ref, out.at[:, :, cols], sems.at[j])
+
+    @pl.loop(0, first)
+    def _(j):
+        store(j, xbuf.at[j]).start()
+
+    @pl.when(solves)
+    def _():
+        last[:, 0] = xbuf[first:, 0]
+
+    both = jnp.concatenate([sent[first], sent[first + 1]], axis=1)
+
+    @pl.loop(jnp.where(solves, 1, 0), cycles)
+    def _(cycle):
+        rows = pl.ds(pl.multiple_of(cycle * tile, tile), tile)
+        delta = jnp.dot(fbuf[rows, :], both, preferred_element_type=jnp.float32)
+        last[0, cycle] = xbuf[first, cycle] - delta[:, :lanes]
+        last[1, cycle] = xbuf[first + 1, cycle] - delta[:, lanes:]
+
+    for i in range(2):
+        store(first + i, last.at[i]).start()
 
     @pl.loop(0, chunks)
     def _(j):
-        store(j).start()
-
-    @pl.loop(0, chunks)
-    def _(j):
-        store(j).wait()
+        store(j, xbuf.at[j]).wait()
 
 
 def local(rhs, factor, inverses):
@@ -402,14 +420,17 @@
     units = chunks * PARTS
     bf16, f32 = jnp.bfloat16, jnp.float32
     dma = lambda n: pltpu.SemaphoreType.DMA((n,))
+    vmem = pl.BlockSpec(memory_space=pltpu.VMEM)
     state = pl.pallas_call(
         functools.partial(kernel, count),
-        out_shape=pltpu.VMEM((chunks, cycles, tile, LANES), f32),
-        in_specs=[pl.BlockSpec(memory_space=pltpu.HBM)] * 3,
-        out_specs=pl.BlockSpec(memory_space=pltpu.VMEM),
-        scratch_shapes=[
+        out_shape=(
+            pltpu.VMEM((chunks, cycles, tile, LANES), f32),
             pltpu.VMEM((chunks, panels * tile, LANES), bf16),
             pltpu.VMEM((cycles * tile, panels * tile), bf16),
+        ),
+        in_specs=[pl.BlockSpec(memory_space=pltpu.HBM)] * 3,
+        out_specs=(vmem, vmem, vmem),
+        scratch_shapes=[
             pltpu.VMEM(factor.shape, bf16),
             pltpu.VMEM((tile, tile), f32),
             pltpu.VMEM((tile, tile), bf16),
@@ -418,19 +439,19 @@
             pltpu.SemaphoreType.DMA, dma(chunks),
         ] + [dma(units)] * 12,
         compiler_params=pltpu.CompilerParams(
-            collective_id=0, has_side_effects=True, vmem_limit_bytes=55 << 20
+            collective_id=0, has_side_effects=True, vmem_limit_bytes=43 << 20
         ),
         name="substitute",
     )(rhs, factor, inverses)
     return pl.pallas_call(
-        place_out,
+        functools.partial(finish, panels),
         out_shape=jax.ShapeDtypeStruct(rhs.shape, f32),
-        in_specs=[pl.BlockSpec(memory_space=pltpu.VMEM)],
+        in_specs=[vmem] * 3,
         out_specs=pl.BlockSpec(memory_space=pl.ANY),
-        scratch_shapes=[dma(chunks)],
+        scratch_shapes=[pltpu.VMEM((2, cycles, tile, LANES), f32), dma(chunks)],
         compiler_params=pltpu.CompilerParams(vmem_limit_bytes=16 << 20),
-        name="place_out",
-    )(state)
+        name="finish",
+    )(*state)
 
 
 def solution(mesh):

time: 103 us -> 102 us (level)
  Pallas kernels: 102 us -> 100 us
    pallas_call x2, Pallas kernels: 102 us -> 100 us  [the longest x1 97 us: local(): pl.pallas_call(functools.partial(kernel, count), out_shape=(pltpu.VMEM((c...]
where the time goes in v6:
time: 102 us; the launch traced here: 100 us
  Pallas kernels  100 us (98%)
    pallas_call x1, Pallas kernels, local(): pl.pallas_call(functools.partial(kernel, count), out_shape=(pltpu.VMEM((c...  97 us
    pallas_call x1, Pallas kernels, local(): pl.pallas_call(functools.partial(finish, panels), out_shape=jax.ShapeDtyp...  3.43 us

profile of v6, /device:TPU:24, one launch (start us, length us, event | category | flops | bytes accessed | tf_op | source)
XLA Modules:
  0.0 100.5 jit_solution(3349642032070446929)
XLA Ops:
  0.0 97.0 %substitute.1 = (f32[16,2,512,128]{3,2,1,0:T(8,128)S(1)}, bf16[16,2048,128]{2,1,0:T(8,128)(2,1)S(1)}, bf16[1024,2048]{1,0:T(8,128)(2,1)S(1)}) custom-call(f32[2,512,2048]{2,1,0:T(8,128)} %rhs.1, bf16[2,512,4,256]{3,2,1,0:T(4,128)(2,1)} %fac.1, f32[4,512,512]{2,1,0:T(8,128)} %inv.1), custom_call_target="tpu_custom_call" | custom-call | tf_op jit(solution)/shard_map/substitute/pallas_call | solution.py:424
  97.0 3.4 %finish.1 = f32[2,512,2048]{2,1,0:T(8,128)} custom-call(f32[16,2,512,128]{3,2,1,0:T(8,128)S(1)} %get-tuple-element.8.xbuf, bf16[16,2048,128]{2,1,0:T(8,128)(2,1)S(1)} %get-tuple-element.9.sent, bf16[1024,2048]{1,0:T(8,128)(2,1)S(1)} %get-tuple-element.10.fbuf), custom_call_target="tpu_custom_call" | custom-call | tf_op jit(solution)/shard_map/finish/pallas_call | solution.py:446

commit v7 on v6

--- a/solution.py
+++ b/solution.py
@@ -11,22 +11,23 @@
 PARTS = 2
 SHARE = 10
 FIRST = (
-    (111366568, 690180661, 689478214, 306485809, 219730482, 304427673, 689543878, 843889201, 415863912, 289743581, 443328081, 308614302, 577845404, 311277202, 460441307, 1073741795, 1073741823),
-    (891316800, 891316800, 891316800, 723544640, 307925190, 81105090, 323697219, 416579866, 891316936, 379859154, 488736531, 327788182, 324089043, 323827859, 443131155, 1073741795, 1073741823),
-    (136314880, 809769858, 145171013, 157387650, 143405426, 288218248, 97030702, 140609731, 97026930, 407147291, 187460277, 439143770, 601167477, 893752856, 460437219, 1073741795, 1073741823),
-    (17043520, 407179329, 721986101, 856203366, 778376261, 423690308, 36209205, 858270067, 79266901, 5714570, 36330698, 895812979, 47547476, 36334282, 725946795, 1073741798, 1073741823),
+    (111366568, 152621109, 152621453, 178594189, 136741718, 105489006, 463672147, 154412425, 437818515, 826594450, 423182930, 309184147, 325960858, 460211931, 594396315, 1073741795, 1073741823),
+    (891316800, 891316800, 891507200, 138504768, 11306542, 421179507, 414746501, 407735176, 319399281, 459926082, 460184640, 308913947, 342733979, 340337812, 306783508, 1073741796, 1073741823),
+    (134479872, 839130000, 144908813, 410313792, 438668177, 833130924, 285490065, 35757277, 271353768, 893766749, 188240968, 288122410, 288098205, 594425589, 477214428, 1073741795, 1073741823),
+    (289706568, 45655553, 169102537, 172004250, 2835800, 173302297, 178397747, 353898705, 56170696, 408235085, 105219488, 306655338, 402742464, 45142421, 768410931, 1073741797, 1073741823),
 )
 ABOVE = (
-    (13897024, 17256501, 30675061, 352591169, 245896206, 168251472, 174431568, 74403906, 35724610, 40416373, 286372776, 292350481, 342176401, 290559699, 441001179, 457848540, 1066252059),
-    (136532488, 148144693, 891325768, 136532488, 315916853, 320509451, 892082328, 276467800, 4595922, 688687017, 306309710, 64259683, 444240579, 309404882, 575485666, 476685971, 1065985746),
-    (18874368, 841505922, 776012365, 845230152, 341914181, 407638952, 845222770, 270833861, 273443480, 424415790, 54715092, 177019634, 189108592, 860989298, 153543893, 499992217, 1066252059),
-    (136348160, 189010440, 54533466, 438652250, 436493505, 170024144, 97289808, 856265810, 231543013, 3335706, 97322632, 194458714, 2972881, 175184794, 859939187, 778385549, 1066067610),
+    (13896576, 673402933, 19091526, 178524557, 675834374, 51990658, 850067701, 306297728, 170449992, 287650507, 405411464, 442805482, 421860451, 457513106, 439203043, 474846434, 1066252059),
+    (148151625, 134244928, 103025705, 688149005, 405602480, 44374920, 406106312, 86087593, 52638233, 13542099, 307600534, 55518297, 374712961, 575354083, 340731099, 577357539, 1065985299),
+    (20971520, 35709265, 365498738, 845197384, 380436613, 499234072, 347668506, 269323138, 776524186, 348427482, 556634205, 319294346, 342799241, 189486801, 866690931, 159683291, 1065726556),
+    (17076224, 17604680, 424436570, 37863598, 816656755, 188748386, 38547883, 438420806, 52506966, 688669934, 432330398, 422652826, 107832665, 365797461, 22647371, 711304514, 1065697958),
 )
-X_FIRST = (0xf77f124, 0xdf7fdd71, 0x1e5eef, 0x820ceafe)
-Y_FIRST = (0xf0880edb, 0x2080228e, 0xffe1a110, 0x7df31501)
-X_ABOVE = (0x18e64004, 0xee9b4821, 0x88868a1, 0x23043300)
-Y_ABOVE = (0x2008289, 0x542, 0xb672120c, 0xdc78cc00)
-U_ABOVE = (0xe5193d72, 0x1164b29c, 0x41058552, 0x8300ff)
+X_FIRST = (0xffde842a, 0xf44c0150, 0x560b52ff, 0x80058805)
+Y_FIRST = (0x216095, 0x28a3, 0xa9f4ad00, 0x74021000)
+X_ABOVE = (0x28f58fa2, 0xefff6e08, 0x40e24a, 0x148546be)
+Y_ABOVE = (0x14023045, 0x10009084, 0xbb3e0531, 0x6b7ab940)
+U_ABOVE = (0xc3084018, 0x173, 0x44811884, 0x80000001)
+D_FIRST = (0x1b40, 0xbb3d60c, 0x0, 0xbf867fa)
 
 
 def pick(place, values):
@@ -48,7 +49,7 @@
 def kernel(count, rhs, fac, inv, xbuf, sent, fbuf, fraw, ibuf, ihigh, ilow,
            f_in, f_send, f_recv, i_in, x_in,
            own_recv, a_recv, b_recv, d_recv,
-           x_send, y_send, next_send, prev_send, rx_send, ry_send, rn_send, rp_send):
+           x_send, y_send, next_send, prev_send, rx_send, ry_send, rn_send, rp_send, rd_send):
     chunks, cycles, tile, lanes = xbuf.shape
     panels = inv.shape[0]
     kpart = fac.shape[3]
@@ -78,11 +79,15 @@
     at_source = {"rows": source * panels + c, "rhs": core}
     early = solves & (c == 0)
 
+    at_bottom = {"rows": c, "rhs": core}
+    at_first = {"rows": jnp.where(planes > 1, panels, 0) + c, "rhs": core}
+
     def table(first, above, place):
         return jnp.where(solves, pick(place, first), pick(place, above))
 
     x_mask = table([signed(m) for m in X_FIRST], [signed(m) for m in X_ABOVE], n1)
     y_mask = table([signed(m) for m in Y_FIRST], [signed(m) for m in Y_ABOVE], n2)
+    d_mask = jnp.where(z == 1, pick(c, [signed(m) for m in D_FIRST]), 0)
     u_mask = jnp.where(to_next | to_prev, pick(c, [signed(m) for m in U_ABOVE]), 0)
 
     def bit(mask, k):
@@ -133,6 +138,7 @@
     relay_x = lambda k: hop(n2, k, rx_send, d_recv, to_n1)
     relay_y = lambda k: hop(n1, k, ry_send, d_recv, to_n2)
     relay_next = lambda k: hop(across, k, rn_send, d_recv, at_next)
+    relay_down = lambda k: hop(across, k, rd_send, d_recv, at_bottom)
     relay_prev = lambda k: hop(across, k, rp_send, d_recv, at_prev)
     arrive_a = lambda k: hop(n1, k, x_send, a_recv, to_n1)
     arrive_b = lambda k: hop(n2, k, y_send, b_recv, to_n2)
@@ -142,7 +148,11 @@
     for to in (to_core, to_n1, to_n2):
         pl.semaphore_signal(barrier, inc=1, device_id=to)
 
-    for on, to in ((to_next, at_next), (to_prev, at_prev), (z > 0, at_source)):
+    apart = middle > 1
+    for on, to in (
+        (to_next, at_next), (to_prev, at_prev), (z > 0, at_source),
+        (solves & apart, at_first), ((z == 1) & apart, at_bottom),
+    ):
         @pl.when(on)
         def _():
             pl.semaphore_signal(barrier, inc=1, device_id=to)
@@ -152,12 +162,18 @@
         i_load().start()
 
     x_load(0).start()
-    for cycle in range(cycles):
-        f_load(cycle).start()
-
-    @pl.loop(1, chunks)
-    def _(j):
-        x_load(j).start()
+
+    def load_rest():
+        for cycle in range(cycles):
+            f_load(cycle).start()
+
+        @pl.loop(1, chunks)
+        def _(j):
+            x_load(j).start()
+
+    @pl.when(jnp.logical_not(early))
+    def _():
+        load_rest()
 
     def f_wait(cycle):
         for p in range(panels):
@@ -193,6 +209,7 @@
     @pl.when(early)
     def _():
         solve(0, 0)
+        load_rest()
 
     @pl.when(jnp.logical_not(early))
     def _():
@@ -201,7 +218,9 @@
 
     words = [table([row[w] for row in FIRST], [row[w] for row in ABOVE], c) for w in range(len(FIRST[0]))]
     pl.semaphore_wait(
-        barrier, 3 + jnp.where(to_next, 1, 0) + jnp.where(to_prev, 1, 0) + jnp.where(z > 0, 1, 0)
+        barrier,
+        3 + jnp.where(to_next, 1, 0) + jnp.where(to_prev, 1, 0) + jnp.where(z > 0, 1, 0)
+        + jnp.where((z < 2) & apart, 1, 0),
     )
 
     @pl.when(jnp.logical_not(early))
@@ -282,6 +301,10 @@
             def _():
                 relay_prev(k).start()
 
+            @pl.when(bit(d_mask, k))
+            def _():
+                relay_down(k).start()
+
         @pl.when(solves & (p < c) & (k % PARTS == PARTS - 1))
         def _():
             correct(p, k // PARTS)
@@ -371,6 +394,10 @@
         @pl.when(bit(u_mask, k) & to_prev)
         def _():
             relay_prev(k).wait_send()
+
+        @pl.when(bit(d_mask, k))
+        def _():
+            relay_down(k).wait_send()
 
     for cycle in range(cycles):
         for p in range(panels):
@@ -437,7 +464,7 @@
             pltpu.VMEM((tile, tile), bf16),
             dma(cycles), dma(cycles * panels), dma(cycles * panels),
             pltpu.SemaphoreType.DMA, dma(chunks),
-        ] + [dma(units)] * 12,
+        ] + [dma(units)] * 13,
         compiler_params=pltpu.CompilerParams(
             collective_id=0, has_side_effects=True, vmem_limit_bytes=43 << 20
         ),

time: 102 us -> 101 us (level)
  no operation moved by 1% of the time
where the time goes in v7:
time: 101 us; the launch traced here: 99.5 us
  Pallas kernels  99.5 us (99%)
    pallas_call x1, Pallas kernels, local(): pl.pallas_call(functools.partial(kernel, count), out_shape=(pltpu.VMEM((c...  96.1 us
    pallas_call x1, Pallas kernels, local(): pl.pallas_call(functools.partial(finish, panels), out_shape=jax.ShapeDtyp...  3.43 us

profile of v7, /device:TPU:24, one launch (start us, length us, event | category | flops | bytes accessed | tf_op | source)
XLA Modules:
  0.0 99.5 jit_solution(6490990545125735458)
XLA Ops:
  0.0 96.1 %substitute.1 = (f32[16,2,512,128]{3,2,1,0:T(8,128)S(1)}, bf16[16,2048,128]{2,1,0:T(8,128)(2,1)S(1)}, bf16[1024,2048]{1,0:T(8,128)(2,1)S(1)}) custom-call(f32[2,512,2048]{2,1,0:T(8,128)} %rhs.1, bf16[2,512,4,256]{3,2,1,0:T(4,128)(2,1)} %fac.1, f32[4,512,512]{2,1,0:T(8,128)} %inv.1), custom_call_target="tpu_custom_call" | custom-call | tf_op jit(solution)/shard_map/substitute/pallas_call | solution.py:451
  96.1 3.4 %finish.1 = f32[2,512,2048]{2,1,0:T(8,128)} custom-call(f32[16,2,512,128]{3,2,1,0:T(8,128)S(1)} %get-tuple-element.8.xbuf, bf16[16,2048,128]{2,1,0:T(8,128)(2,1)S(1)} %get-tuple-element.9.sent, bf16[1024,2048]{1,0:T(8,128)(2,1)S(1)} %get-tuple-element.10.fbuf), custom_call_target="tpu_custom_call" | custom-call | tf_op jit(solution)/shard_map/finish/pallas_call | solution.py:473

commit v8 on v7

--- a/solution.py
+++ b/solution.py
@@ -309,6 +309,35 @@
         def _():
             correct(p, k // PARTS)
 
+    def drain(k):
+        @pl.when(to_next)
+        def _():
+            own_next(k).wait_send()
+
+        @pl.when(to_prev)
+        def _():
+            own_prev(k).wait_send()
+
+        @pl.when(bit(x_mask, k))
+        def _():
+            relay_x(k).wait_send()
+
+        @pl.when(bit(y_mask, k))
+        def _():
+            relay_y(k).wait_send()
+
+        @pl.when(bit(u_mask, k) & to_next)
+        def _():
+            relay_next(k).wait_send()
+
+        @pl.when(bit(u_mask, k) & to_prev)
+        def _():
+            relay_prev(k).wait_send()
+
+        @pl.when(bit(d_mask, k))
+        def _():
+            relay_down(k).wait_send()
+
     def update(u):
         @pl.when(u == 0)
         def _():
@@ -335,6 +364,12 @@
             def _():
                 take(p, at[p])
 
+        @pl.when((symbol == 4) & (us > 1))
+        def _():
+            @pl.loop(0, 2 * PARTS)
+            def _(i):
+                drain((us - 2) * 2 * PARTS + i)
+
         @pl.when((symbol == 4) & (us < chunks // 2 - 1))
         def _():
             update(us)
@@ -371,33 +406,9 @@
         own_x(k).wait_send()
         own_y(k).wait_send()
 
-        @pl.when(to_next)
-        def _():
-            own_next(k).wait_send()
-
-        @pl.when(to_prev)
-        def _():
-            own_prev(k).wait_send()
-
-        @pl.when(bit(x_mask, k))
-        def _():
-            relay_x(k).wait_send()
-
-        @pl.when(bit(y_mask, k))
-        def _():
-            relay_y(k).wait_send()
-
-        @pl.when(bit(u_mask, k) & to_next)
-        def _():
-            relay_next(k).wait_send()
-
-        @pl.when(bit(u_mask, k) & to_prev)
-        def _():
-            relay_prev(k).wait_send()
-
-        @pl.when(bit(d_mask, k))
-        def _():
-            relay_down(k).wait_send()
+    @pl.loop((chunks - 4) * PARTS, chunks * PARTS)
+    def _(k):
+        drain(k)
 
     for cycle in range(cycles):
         for p in range(panels):

time: 101 us -> 101 us (level)
  the two profiles are of different devices: /device:TPU:24 before, /device:TPU:2 now
where the time goes in v8:
time: 101 us
  Pallas kernels  101 us (100%)
    pallas_call x1, Pallas kernels, local(): pl.pallas_call(functools.partial(kernel, count), out_shape=(pltpu.VMEM((c...  97.6 us
    pallas_call x1, Pallas kernels, local(): pl.pallas_call(functools.partial(finish, panels), out_shape=jax.ShapeDtyp...  3.43 us

profile of v8, /device:TPU:2, one launch (start us, length us, event | category | flops | bytes accessed | tf_op | source)
XLA Modules:
  0.0 101.1 jit_solution(8906236947992838095)
XLA Ops:
  0.0 97.6 %substitute.1 = (f32[16,2,512,128]{3,2,1,0:T(8,128)S(1)}, bf16[16,2048,128]{2,1,0:T(8,128)(2,1)S(1)}, bf16[1024,2048]{1,0:T(8,128)(2,1)S(1)}) custom-call(f32[2,512,2048]{2,1,0:T(8,128)} %rhs.1, bf16[2,512,4,256]{3,2,1,0:T(4,128)(2,1)} %fac.1, f32[4,512,512]{2,1,0:T(8,128)} %inv.1), custom_call_target="tpu_custom_call" | custom-call | tf_op jit(solution)/shard_map/substitute/pallas_call | solution.py:462
  97.7 3.4 %finish.1 = f32[2,512,2048]{2,1,0:T(8,128)} custom-call(f32[16,2,512,128]{3,2,1,0:T(8,128)S(1)} %get-tuple-element.8.xbuf, bf16[16,2048,128]{2,1,0:T(8,128)(2,1)S(1)} %get-tuple-element.9.sent, bf16[1024,2048]{1,0:T(8,128)(2,1)S(1)} %get-tuple-element.10.fbuf), custom_call_target="tpu_custom_call" | custom-call | tf_op jit(solution)/shard_map/finish/pallas_call | solution.py:484

commit v9 on v8

--- a/solution.py
+++ b/solution.py
@@ -310,6 +310,9 @@
             correct(p, k // PARTS)
 
     def drain(k):
+        own_x(k).wait_send()
+        own_y(k).wait_send()
+
         @pl.when(to_next)
         def _():
             own_next(k).wait_send()
@@ -400,11 +403,6 @@
 
     zero = jnp.int32(0)
     lax.fori_loop(0, len(words), stride, ((zero,) * panels, zero, zero, zero))
-
-    @pl.loop(0, chunks * PARTS)
-    def _(k):
-        own_x(k).wait_send()
-        own_y(k).wait_send()
 
     @pl.loop((chunks - 4) * PARTS, chunks * PARTS)
     def _(k):

time: 101 us -> 101 us (level)
  no operation moved by 1% of the time
where the time goes in v9:
time: 101 us
  Pallas kernels  101 us (100%)
    pallas_call x1, Pallas kernels, local(): pl.pallas_call(functools.partial(kernel, count), out_shape=(pltpu.VMEM((c...  97.5 us
    pallas_call x1, Pallas kernels, local(): pl.pallas_call(functools.partial(finish, panels), out_shape=jax.ShapeDtyp...  3.43 us

profile of v9, /device:TPU:2, one launch (start us, length us, event | category | flops | bytes accessed | tf_op | source)
XLA Modules:
  0.0 100.9 jit_solution(2385598974457315620)
XLA Ops:
  0.0 97.5 %substitute.1 = (f32[16,2,512,128]{3,2,1,0:T(8,128)S(1)}, bf16[16,2048,128]{2,1,0:T(8,128)(2,1)S(1)}, bf16[1024,2048]{1,0:T(8,128)(2,1)S(1)}) custom-call(f32[2,512,2048]{2,1,0:T(8,128)} %rhs.1, bf16[2,512,4,256]{3,2,1,0:T(4,128)(2,1)} %fac.1, f32[4,512,512]{2,1,0:T(8,128)} %inv.1), custom_call_target="tpu_custom_call" | custom-call | tf_op jit(solution)/shard_map/substitute/pallas_call | solution.py:460
  97.5 3.4 %finish.1 = f32[2,512,2048]{2,1,0:T(8,128)} custom-call(f32[16,2,512,128]{3,2,1,0:T(8,128)S(1)} %get-tuple-element.8.xbuf, bf16[16,2048,128]{2,1,0:T(8,128)(2,1)S(1)} %get-tuple-element.9.sent, bf16[1024,2048]{1,0:T(8,128)(2,1)S(1)} %get-tuple-element.10.fbuf), custom_call_target="tpu_custom_call" | custom-call | tf_op jit(solution)/shard_map/finish/pallas_call | solution.py:482
